TPU v7x, 32 devices: a whole 2x2x4 slice. The times are simulated.
32 devices in a mesh: seq: 16 (over z, y, core), head: 2 (over x).
Axes of the slice: x: 2, y: 2, z: 4, core: 2. Of those that a mesh axis runs over, the one named last changes fastest.
Arguments:
- queries: bfloat16 [2048, 2048], P('seq', 'head'), may hold values from -190 to 190
- key_vectors: bfloat16 [2048, 256], P('seq', 'head'), may hold values from -6.1 to 6.1
- value_vectors: bfloat16 [2048, 256], P('seq', 'head'), may hold values from -54 to 54
- log_gate: float32 [16, 2048], P('head', 'seq'), may hold values from -1 to 0, as said below
- query_map: float32 [16, 128, 128], P('head'), may hold values from -0.5 to 0.5
- key_map: float32 [16, 128, 128], P('head'), may hold values from -0.5 to 0.5
- level_weight: float32 [16, 12], P('head'), may hold values from 0.25 to 2
- norm_gain: float32 [2048], P('head'), may hold values from 0.5 to 1.5
Outputs:
- grad_query_map: float32 [16, 128, 128], P('head')
- grad_key_map: float32 [16, 128, 128], P('head')
- grad_level_weight: float32 [16, 12], P('head')
- grad_norm_gain: float32 [2048], P('head')
Inputs may be any that keep to these rules, and one draw needn't show every extreme that they name: `log_gate`: every entry is negative.
All inputs are finite; a program needn't handle non-finite values.
Results may differ from a plain program's by a relative error of at most 0.0015.
Values may be sent and summed in bfloat16 or wider, within the bound.
No kernel may reach another device: no remote copies, remote signals or barrier semaphores. Data moves between devices by JAX's collectives and lax.ppermute only.
A program may use at most 128 MiB of HBM per device.

v0:
```python
import jax
import jax.numpy as jnp
from jax import lax
from jax.sharding import PartitionSpec as P

HIGHEST = lax.Precision.HIGHEST
NEGATIVE = -1e30
EPSILON = 1e-05


def carried_in(value, axis, join, neutral):
    count, mine = (lax.axis_size(axis), lax.axis_index(axis))
    pieces = lax.all_gather(value, axis)
    subtotal = jnp.full_like(value, 0) + jnp.asarray(neutral, value.dtype)

    def hop(position, subtotal):
        longer = join(subtotal, pieces[position])
        return jnp.where(position < mine, longer, subtotal)

    return lax.fori_loop(0, count - 1, hop, subtotal)


def bit_length(numbers, bit_count):
    digits = jnp.zeros_like(numbers)
    for bit_power in range(bit_count):
        digits = digits + (numbers >= 1 << bit_power).astype(jnp.int32)
    return digits


def teacher_target(query_rows, key_rows, value_rows, first_row):
    span_rows, head_count, head_dim = query_rows.shape
    score_scale = head_dim ** (-0.5)
    positions = first_row + lax.iota(jnp.int32, span_rows)
    row_peak = jnp.full((head_count, span_rows), NEGATIVE, jnp.float32)
    key_piece = lax.all_gather(key_rows, "seq", axis=0, tiled=True)
    value_piece = lax.all_gather(value_rows, "seq", axis=0, tiled=True)
    scores = (
        jnp.einsum("rgd,kd->grk", query_rows, key_piece, preferred_element_type=jnp.float32)
        * score_scale
    )
    key_pos = lax.iota(jnp.int32, key_piece.shape[0])
    scores = jnp.where(key_pos[None, None, :] <= positions[None, :, None], scores, NEGATIVE)
    new_peak = jnp.maximum(row_peak, jnp.max(scores, axis=2))
    weights = jnp.exp(scores - new_peak[..., None])
    update = jnp.einsum(
        "grk,kd->grd", weights.astype(jnp.bfloat16), value_piece, preferred_element_type=jnp.float32
    )
    row_total = jnp.sum(weights, axis=2)
    return update / row_total[..., None]


def fenwick_gathered(raw_state, ending, before, span_id, span_bits):
    initial = jnp.zeros((span_bits,) + raw_state.shape, jnp.float32)
    piece_states = lax.all_gather(raw_state[None], "seq", axis=0, tiled=True)
    piece_ends = lax.all_gather(ending[None], "seq", axis=0, tiled=True)
    piece_count = piece_states.shape[0]
    source_id = lax.iota(jnp.int32, piece_count)
    level_id = bit_length(jnp.bitwise_xor(source_id, span_id), span_bits)
    earlier = source_id < span_id
    exponent = jnp.where(earlier[:, None], before[None, :] - piece_ends, NEGATIVE)
    link_decay = jnp.exp(exponent)
    level_pick = (level_id[:, None] == (1 + lax.iota(jnp.int32, span_bits))[None, :]).astype(
        jnp.float32
    )
    coupling = level_pick[:, :, None] * link_decay[:, None, :]
    return initial + jnp.einsum("njg,ngab->jgab", coupling, piece_states, precision=HIGHEST)


def on_device(
    queries, key_vectors, value_vectors, log_gate, query_map, key_map, level_weight, norm_gain
):
    span_rows, head_dim = key_vectors.shape
    head_count = queries.shape[1] // head_dim
    seq_count = lax.axis_size("seq")
    span_id = lax.axis_index("seq")
    span_bits = seq_count.bit_length() - 1
    low_bits = span_rows.bit_length() - 1
    total_tokens = span_rows * seq_count
    norm_width = head_count * head_dim * lax.axis_size("head")
    query_rows = queries.reshape(span_rows, head_count, head_dim)
    target = teacher_target(query_rows, key_vectors, value_vectors, span_id * span_rows)
    local_cum = jnp.cumsum(log_gate, axis=1)
    before = carried_in(
        local_cum[:, -1],
        "seq",
        lambda earlier, later_term: earlier + later_term,
        jnp.zeros((head_count,), jnp.float32),
    )
    cumulative = before[:, None] + local_cum
    ending = cumulative[:, -1]
    query_float = query_rows.astype(jnp.float32)
    keys_float = key_vectors.astype(jnp.float32)
    values_float = value_vectors.astype(jnp.float32)
    query_proj = jnp.einsum("rgd,gde->gre", query_float, query_map, precision=HIGHEST)
    key_proj = jnp.einsum("rd,gde->gre", keys_float, key_map, precision=HIGHEST)
    position = lax.iota(jnp.int32, span_rows)
    causal = position[None, :] <= position[:, None]
    local_level = bit_length(jnp.bitwise_xor(position[:, None], position[None, :]), low_bits)
    decay_in = jnp.exp(
        jnp.where(causal[None], cumulative[:, :, None] - cumulative[:, None, :], NEGATIVE)
    )
    level_mask = jnp.zeros_like(decay_in)
    for level_id in range(low_bits + 1):
        level_mask = (
            level_mask
            + level_weight[:, level_id][:, None, None]
            * (local_level == level_id).astype(jnp.float32)[None]
        )
    mix_weight = decay_in * level_mask
    scores = jnp.einsum("gre,gse->grs", query_proj, key_proj, precision=HIGHEST)
    local_part = jnp.einsum("grs,sd->grd", scores * mix_weight, values_float, precision=HIGHEST)
    raw_state = jnp.einsum(
        "gsa,sb->gab",
        jnp.exp(ending[:, None] - cumulative)[:, :, None] * keys_float[None],
        values_float,
        precision=HIGHEST,
    )
    level_states = fenwick_gathered(raw_state, ending, before, span_id, span_bits)
    cross_weight = level_weight[:, low_bits + 1 :]
    combined = jnp.einsum("gj,jgab->gab", cross_weight, level_states, precision=HIGHEST)
    key_state = jnp.einsum("gba,gbf->gaf", key_map, combined, precision=HIGHEST)
    entry_decay = jnp.exp(cumulative - before[:, None])
    far_part = entry_decay[:, :, None] * jnp.einsum(
        "gre,gef->grf", query_proj, key_state, precision=HIGHEST
    )
    student_raw = local_part + far_part
    square_sum = lax.psum(jnp.sum(student_raw * student_raw, axis=(0, 2)), "head")
    inverse = lax.rsqrt(square_sum / norm_width + EPSILON)
    gain_rows = norm_gain.reshape(head_count, 1, head_dim)
    normed = student_raw * inverse[None, :, None]
    mismatch = (normed * gain_rows - target) / total_tokens
    grad_gain = jnp.sum(mismatch * normed, axis=1).reshape(-1)
    scaled_cot = mismatch * gain_rows
    inner_sum = lax.psum(jnp.sum(scaled_cot * student_raw, axis=(0, 2)), "head")
    residual = (
        inverse[None, :, None] * scaled_cot
        - student_raw * (inverse * inverse * inverse * inner_sum / norm_width)[None, :, None]
    )
    d_mix = jnp.einsum("grd,sd->grs", residual, values_float, precision=HIGHEST)
    d_scores = d_mix * mix_weight
    through = d_mix * scores * decay_in
    local_grads = [
        jnp.sum(through * (local_level == level_id).astype(jnp.float32)[None], axis=(1, 2))
        for level_id in range(low_bits + 1)
    ]
    d_state = jnp.einsum(
        "gre,grf->gef", entry_decay[:, :, None] * query_proj, residual, precision=HIGHEST
    )
    d_combined = jnp.einsum("gba,gaf->gbf", key_map, d_state, precision=HIGHEST)
    d_query = jnp.einsum("grs,gse->gre", d_scores, key_proj, precision=HIGHEST) + entry_decay[
        :, :, None
    ] * jnp.einsum("grf,gef->gre", residual, key_state, precision=HIGHEST)
    d_key = jnp.einsum("grs,gre->gse", d_scores, query_proj, precision=HIGHEST)
    grad_query = jnp.einsum("rgb,gre->gbe", query_float, d_query, precision=HIGHEST)
    grad_key = jnp.einsum("gbf,gaf->gba", combined, d_state, precision=HIGHEST) + jnp.einsum(
        "rb,gre->gbe", keys_float, d_key, precision=HIGHEST
    )
    cross_grads = jnp.einsum("jgab,gab->gj", level_states, d_combined, precision=HIGHEST)
    grad_levels = jnp.concatenate([jnp.stack(local_grads, axis=1), cross_grads], axis=1)
    return lax.psum((grad_query, grad_key, grad_levels, grad_gain), "seq")


def solution(mesh):
    placed = (
        P("seq", "head"),
        P("seq", "head"),
        P("seq", "head"),
        P("head", "seq"),
        P("head", None, None),
        P("head", None, None),
        P("head", None),
        P("head"),
    )
    return jax.shard_map(
        on_device,
        mesh=mesh,
        in_specs=placed,
        out_specs=(P("head", None, None), P("head", None, None), P("head", None), P("head")),
        check_vma=False,
    )
```

profile of v0, /device:TPU:0, one launch (start us, length us, event | category | flops | bytes accessed | tf_op | source)
XLA Modules:
  0.0 298.1 jit_solution(158469904230548614)
XLA Ops:
  7.3 1.0 reduce_window_sum.11
  8.3 0.2 slice_reduce_fusion.9
  8.4 1.2 dynamic-slice
  10.3 0.2 dynamic-update-slice
  10.6 34.9 %all-reduce = f32[128]{0:T(128)S(1)} all-reduce(f32[128]{0:T(128)S(1)} %dynamic-update-slice), channel_id=2, replica_groups=mesh['seq'=16,'head'=2] {'seq'}, use_global_device_ids=true, to_apply=%add | all-reduce | flops 128 | bytes 1024
  45.5 0.1 reshape.329
  45.6 0.6 while.14
  46.3 0.2 slice_reduce_fusion
  46.5 0.1 subtract_exponential_fusion.1
  46.6 0.9 copy.116
  47.4 1.9 fusion.25
  49.4 0.8 slice.46
  50.2 0.2 dynamic-update-slice.1
  50.4 30.4 %all-reduce.1 = f32[128]{0:T(128)S(1)} all-reduce(f32[128]{0:T(128)S(1)} %dynamic-update-slice.1), channel_id=4, replica_groups=mesh['seq'=16,'head'=2] {'seq'}, use_global_device_ids=true, to_apply=%add.1 | all-reduce | flops 128 | bytes 1024
  80.8 0.1 reshape.331
  81.0 1.3 slice_reduce_fusion.8
  82.8 0.7 compare_convert_fusion.8
  83.5 0.7 select_exponential_fusion.1
  84.2 22.4 %all_gather.18 = bf16[2048,128]{1,0:T(8,128)(2,1)S(1)} all-gather(bf16[128,128]{1,0:T(8,128)(2,1)} %param.11), channel_id=1, replica_groups=mesh['seq'=16,'head'=2] {'seq'}, dimensions={0}, use_global_device_ids=true | all-gather | bytes 557056 | tf_op jit(solution)/shard_map/all_gather | solution.py:35
  106.5 0.2 iota_compare_fusion
  106.7 2.3 fusion.4
  109.1 0.6 broadcast_multiply_fusion
  109.7 23.8 %all_gather.19 = bf16[2048,128]{1,0:T(8,128)(2,1)} all-gather(bf16[128,128]{1,0:T(8,128)(2,1)S(1)} %copy-done.14), channel_id=1, replica_groups=mesh['seq'=16,'head'=2] {'seq'}, dimensions={0}, use_global_device_ids=true | all-gather | bytes 557056 | tf_op jit(solution)/shard_map/all_gather | solution.py:36
  133.5 0.6 fusion.55
  134.2 0.4 fusion.31
  134.6 0.6 fusion.68
  135.4 1.6 fusion.27
  137.1 2.3 fusion.2
  139.4 12.5 %fusion = f32[8,128,128,4]{2,3,1,0:T(4,128)S(1)} fusion(f32[16,8,128,128]{3,2,1,0:T(8,128)} %bitcast.126, f32[16,8]{0,1:T(8,128)} %select_exponential_fusion.1, f32[16,4]{0,1:T(4,128)} %compare_convert_fusion.8), kind=kOutput, calls=%fused_computation.3 | convolution fusion | flops 100663808 | bytes 10486528 | tf_op jit(solution)/shard_map/njg,ngab->jgab/dot_general | solution.py:66
  151.9 3.8 %fusion.10 = f32[8,1,128,128]{3,1,2,0:T(1,128)S(1)} fusion(f32[8,4,1,1]{1,2,3,0:T(1,128)S(1)} %bitcast.129, f32[8,128,128,4]{2,3,1,0:T(4,128)S(1)} %fusion), kind=kOutput, calls=%fused_computation.13 | convolution fusion | flops 6291456 | bytes 2621568 | tf_op jit(solution)/shard_map/gj,jgab->gab/dot_general | solution.py:120
  155.8 0.8 copy-done.2
  156.6 1.0 fusion.69
  157.6 0.8 copy-done.4
  158.4 2.5 multiply_reduce_fusion.10
  160.9 5.5 %psum.42 = f32[128]{0:T(128)} all-reduce(f32[128]{0:T(128)} %get-tuple-element.153), channel_id=1, replica_groups=mesh['seq'=16,'head'=2] {'head'}, use_global_device_ids=true, to_apply=%region_4.5 | all-reduce | flops 128 | bytes 1024 | tf_op jit(solution)/shard_map/psum | solution.py:127
  166.5 0.6 add_rsqrt_fusion
  167.1 7.1 %multiply_reduce_fusion = (f32[8,128]{1,0:T(8,128)}, f32[128]{0:T(128)}, f32[8,128,128]{2,1,0:T(8,128)}) fusion(f32[8,128,128]{2,1,0:T(8,128)} %get-tuple-element.154, f32[128]{0:T(128)S(1)} %add_rsqrt_fusion, f32[8,128]{1,0:T(8,128)} %get-tuple-element.167, f32[8,128]{1,0:T(8,128)} %fusion.2, bf16[2048,128]{1,0:T(8,128)(2,1)} %all_gather.19, ...), kind=kOutput, calls=%fused_computation.29 | convolution fusion | flops 546569088 | bytes 10245120 | tf_op jit(solution)/shard_map/grk,kd->grd/dot_general | solution.py:45
  174.2 5.8 %psum.43 = f32[128]{0:T(128)} all-reduce(f32[128]{0:T(128)} %get-tuple-element.120), channel_id=1, replica_groups=mesh['seq'=16,'head'=2] {'head'}, use_global_device_ids=true, to_apply=%region_8.9 | all-reduce | flops 128 | bytes 1024 | tf_op jit(solution)/shard_map/psum | solution.py:134
  180.1 0.8 fusion.65
  180.8 1.3 multiply_subtract_fusion
  182.2 2.7 multiply_reduce_fusion.1
  184.9 2.9 fusion.38
  187.8 2.4 fusion.36
  190.3 1.2 fusion.23
  191.5 0.7 fusion.12
  192.1 0.4 convolution_bitcast_fusion
  192.6 1.4 convolution_bitcast_fusion.1
  194.0 2.0 convolution_add_fusion
  196.0 2.1 convolution_bitcast_fusion.2
  198.1 1.3 copy.155
  199.4 0.1 copy.137
  199.5 0.1 copy.138
  199.6 0.1 copy.136
  199.6 0.1 copy.135
  199.7 0.1 copy.134
  199.8 0.1 copy.133
  199.9 0.1 copy.132
  200.0 0.1 copy.131
  200.1 9.6 %fusion.8 = f32[8,1,4,1]{2,1,3,0:T(1,128)S(1)} fusion(f32[8,128,128,1]{2,3,1,0:T(1,128)} %copy.155, f32[8,128,128,4]{2,3,1,0:T(4,128)S(1)} %fusion), kind=kOutput, calls=%fused_computation.11 | convolution fusion | flops 6291456 | bytes 2621568 | tf_op jit(solution)/shard_map/jgab,gab->gj/dot_general | solution.py:158
  209.7 0.1 concatenate.3
  209.8 30.6 %all-reduce.2 = (f32[8,12]{1,0:T(8,128)}, f32[1024]{0:T(1024)}) all-reduce(f32[8,12]{1,0:T(8,128)S(1)} %concatenate.3, f32[1024]{0:T(1024)S(1)} %bitcast.131), channel_id=1, replica_groups=mesh['seq'=16,'head'=2] {'seq'}, use_global_device_ids=true, to_apply=%region_19.20 | all-reduce | flops 1120 | bytes 8960 | tf_op jit(solution)/shard_map/psum | solution.py:160
  240.4 47.0 %all-reduce.6.cloned.1.call-done = (f32[8,128,128]{1,2,0:T(8,128)}, f32[8,128,128]{2,1,0:T(8,128)}) async-done(((f32[8,128,128]{1,2,0:T(8,128)}, f32[8,128,128]{2,1,0:T(8,128)}), (f32[8,128,128]{1,2,0:T(8,128)}, f32[8,128,128]{2,1,0:T(8,128)})) %all-reduce.6.cloned.1.call-update) | async-done | bytes 1048592 | tf_op jit(solution)/shard_map/psum | solution.py:160
  287.4 2.0 copy.139
  289.4 1.9 copy.186
  (114 shorter events, 1.1 us)
Async XLA Ops:
  7.2 126.4 %copy-start = (f32[8,128,128]{2,1,0:T(8,128)S(1)}, f32[8,128,128]{2,1,0:T(8,128)}, u32[]{:S(2)}) copy-start(f32[8,128,128]{2,1,0:T(8,128)} %param.15) | copy-start | bytes 1572868
  7.2 132.2 %all-gather.5.cloned.1.call-start = ((), (), s32[]{:S(2)}) async-start(), calls=%async_computation | async-start | bytes 8912896 | tf_op jit(solution)/shard_map/all_gather | solution.py:54
  46.2 62.8 %copy-start.25 = (f32[1024]{0:T(1024)S(1)}, f32[1024]{0:T(1024)}, u32[]{:S(2)}) copy-start(f32[1024]{0:T(1024)} %param.17) | copy-start | bytes 12292
  46.2 63.5 %copy-start.14 = (bf16[128,128]{1,0:T(8,128)(2,1)S(1)}, bf16[128,128]{1,0:T(8,128)(2,1)}, u32[]{:S(2)}) copy-start(bf16[128,128]{1,0:T(8,128)(2,1)} %param.12) | copy-start | bytes 98308
  49.4 84.2 %copy-start.12 = (bf16[128,128]{1,0:T(8,128)(2,1)S(1)}, bf16[128,128]{1,0:T(8,128)(2,1)}, u32[]{:S(2)}) copy-start(bf16[128,128]{1,0:T(8,128)(2,1)} %param.11) | copy-start | bytes 98308
  49.4 238.0 %all-reduce.6.cloned.1.call-start = ((), (), s32[]{:S(2)}) async-start(), calls=%async_computation.1 | async-start | bytes 2097152 | tf_op jit(solution)/shard_map/psum | solution.py:160
  82.3 53.0 %copy-start.26 = (f32[8]{0:T(128)}, f32[8]{0:T(128)S(1)}, u32[]{:S(2)}) copy-start(f32[8]{0:T(128)S(1)} %get-tuple-element.129) | copy-start | bytes 100
  82.3 53.0 %copy-start.27 = (f32[8]{0:T(128)}, f32[8]{0:T(128)S(1)}, u32[]{:S(2)}) copy-start(f32[8]{0:T(128)S(1)} %get-tuple-element.130) | copy-start | bytes 100
  82.3 53.0 %copy-start.28 = (f32[8]{0:T(128)}, f32[8]{0:T(128)S(1)}, u32[]{:S(2)}) copy-start(f32[8]{0:T(128)S(1)} %get-tuple-element.131) | copy-start | bytes 100
  82.3 53.0 %copy-start.29 = (f32[8]{0:T(128)}, f32[8]{0:T(128)S(1)}, u32[]{:S(2)}) copy-start(f32[8]{0:T(128)S(1)} %get-tuple-element.132) | copy-start | bytes 100
  82.3 53.0 %copy-start.30 = (f32[8]{0:T(128)}, f32[8]{0:T(128)S(1)}, u32[]{:S(2)}) copy-start(f32[8]{0:T(128)S(1)} %get-tuple-element.133) | copy-start | bytes 100
  82.4 53.0 %copy-start.31 = (f32[8]{0:T(128)}, f32[8]{0:T(128)S(1)}, u32[]{:S(2)}) copy-start(f32[8]{0:T(128)S(1)} %get-tuple-element.134) | copy-start | bytes 100
  82.4 53.0 %copy-start.32 = (f32[8]{0:T(128)}, f32[8]{0:T(128)S(1)}, u32[]{:S(2)}) copy-start(f32[8]{0:T(128)S(1)} %get-tuple-element.135) | copy-start | bytes 100
  82.4 53.0 %copy-start.33 = (f32[8]{0:T(128)}, f32[8]{0:T(128)S(1)}, u32[]{:S(2)}) copy-start(f32[8]{0:T(128)S(1)} %get-tuple-element.136) | copy-start | bytes 100
  82.4 52.9 %copy-start.15 = (f32[128,128]{1,0:T(8,128)}, f32[128,128]{1,0:T(8,128)S(1)}, u32[]{:S(2)}) copy-start(f32[128,128]{1,0:T(8,128)S(1)} %compare_convert_fusion.7) | copy-start | bytes 196612
  82.5 52.8 %copy-start.23 = (pred[128,128]{1,0:T(8,128)(4,1)}, pred[128,128]{1,0:T(8,128)(4,1)S(1)}, u32[]{:S(2)}) copy-start(pred[128,128]{1,0:T(8,128)(4,1)S(1)} %get-tuple-element.159) | copy-start | bytes 49156
  82.6 52.7 %copy-start.16 = (f32[128,128]{1,0:T(8,128)}, f32[128,128]{1,0:T(8,128)S(1)}, u32[]{:S(2)}) copy-start(f32[128,128]{1,0:T(8,128)S(1)} %get-tuple-element.165) | copy-start | bytes 196612
  82.6 52.7 %copy-start.17 = (f32[128,128]{1,0:T(8,128)}, f32[128,128]{1,0:T(8,128)S(1)}, u32[]{:S(2)}) copy-start(f32[128,128]{1,0:T(8,128)S(1)} %get-tuple-element.166) | copy-start | bytes 196612
  82.6 51.5 %copy-start.7 = (bf16[128,1024]{1,0:T(8,128)(2,1)S(1)}, bf16[128,1024]{1,0:T(8,128)(2,1)}, u32[]{:S(2)}) copy-start(bf16[128,1024]{1,0:T(8,128)(2,1)} %param.10) | copy-start | bytes 786436
  82.6 51.5 %copy-start.13 = (f32[8,128,128]{2,1,0:T(8,128)S(1)}, f32[8,128,128]{2,1,0:T(8,128)}, u32[]{:S(2)}) copy-start(f32[8,128,128]{2,1,0:T(8,128)} %param.14) | copy-start | bytes 1572868
  82.7 52.7 %copy-start.18 = (f32[128,128]{1,0:T(8,128)}, f32[128,128]{1,0:T(8,128)S(1)}, u32[]{:S(2)}) copy-start(f32[128,128]{1,0:T(8,128)S(1)} %get-tuple-element.163) | copy-start | bytes 196612
  82.7 52.7 %copy-start.19 = (f32[128,128]{1,0:T(8,128)}, f32[128,128]{1,0:T(8,128)S(1)}, u32[]{:S(2)}) copy-start(f32[128,128]{1,0:T(8,128)S(1)} %get-tuple-element.164) | copy-start | bytes 196612
  82.8 52.6 %copy-start.20 = (f32[128,128]{1,0:T(8,128)}, f32[128,128]{1,0:T(8,128)S(1)}, u32[]{:S(2)}) copy-start(f32[128,128]{1,0:T(8,128)S(1)} %get-tuple-element.161) | copy-start | bytes 196612
  82.8 52.6 %copy-start.21 = (f32[128,128]{1,0:T(8,128)}, f32[128,128]{1,0:T(8,128)S(1)}, u32[]{:S(2)}) copy-start(f32[128,128]{1,0:T(8,128)S(1)} %get-tuple-element.162) | copy-start | bytes 196612
  109.0 28.0 %copy-start.1 = (f32[2048,128,8]{1,0,2:T(8,128)}, f32[2048,128,8]{1,0,2:T(8,128)S(1)}, u32[]{:S(2)}) copy-start(f32[2048,128,8]{1,0,2:T(8,128)S(1)} %get-tuple-element.152) | copy-start | bytes 25165828
  134.2 5.2 %copy-start.9 = (f32[8,128,128]{2,1,0:T(8,128)}, f32[8,128,128]{2,1,0:T(8,128)S(1)}, u32[]{:S(2)}) copy-start(f32[8,128,128]{2,1,0:T(8,128)S(1)} %fusion.55) | copy-start | bytes 1572868
  135.2 4.2 %copy-start.10 = (f32[8,128,128]{2,1,0:T(8,128)}, f32[8,128,128]{2,1,0:T(8,128)S(1)}, u32[]{:S(2)}) copy-start(f32[8,128,128]{2,1,0:T(8,128)S(1)} %fusion.68) | copy-start | bytes 1572868
  139.4 19.0 %copy-start.11 = (f32[8,128,128]{2,1,0:T(8,128)S(1)}, f32[8,128,128]{2,1,0:T(8,128)}, u32[]{:S(2)}) copy-start(f32[8,128,128]{2,1,0:T(8,128)} %fusion.27) | copy-start | bytes 1572868
  155.8 0.8 copy-start.2
  157.6 0.8 copy-start.4
  160.9 19.9 %copy-start.22 = (f32[8,128]{1,0:T(8,128)S(1)}, f32[8,128]{1,0:T(8,128)}, u32[]{:S(2)}) copy-start(f32[8,128]{1,0:T(8,128)} %get-tuple-element.167) | copy-start | bytes 12292
  167.1 7.1 %copy-start.34 = (f32[128]{0:T(128)}, f32[128]{0:T(128)S(1)}, u32[]{:S(2)}) copy-start(f32[128]{0:T(128)S(1)} %add_rsqrt_fusion) | copy-start | bytes 1540
  174.2 18.3 %copy-start.8 = (bf16[128,1024]{1,0:T(8,128)(2,1)S(1)}, bf16[128,1024]{1,0:T(8,128)(2,1)}, u32[]{:S(2)}) copy-start(bf16[128,1024]{1,0:T(8,128)(2,1)} %param.10) | copy-start | bytes 786436
  180.1 11.4 %copy-start.5 = (f32[8,128,128]{2,1,0:T(8,128)S(1)}, f32[8,128,128]{2,1,0:T(8,128)}, u32[]{:S(2)}) copy-start(f32[8,128,128]{2,1,0:T(8,128)} %copy-done.4) | copy-start | bytes 1572868
  180.1 13.9 %copy-start.3 = (f32[8,1,128,128]{3,1,2,0:T(1,128)S(1)}, f32[8,1,128,128]{3,1,2,0:T(1,128)}, u32[]{:S(2)}) copy-start(f32[8,1,128,128]{3,1,2,0:T(1,128)} %copy-done.2) | copy-start | bytes 1572868
  184.9 14.5 %copy-start.40 = (f32[8]{0:T(128)S(1)}, f32[8]{0:T(128)}, u32[]{:S(2)}) copy-start(f32[8]{0:T(128)} %get-tuple-element.122) | copy-start | bytes 100
  184.9 14.6 %copy-start.39 = (f32[8]{0:T(128)S(1)}, f32[8]{0:T(128)}, u32[]{:S(2)}) copy-start(f32[8]{0:T(128)} %get-tuple-element.121) | copy-start | bytes 100
  184.9 14.6 %copy-start.38 = (f32[8]{0:T(128)S(1)}, f32[8]{0:T(128)}, u32[]{:S(2)}) copy-start(f32[8]{0:T(128)} %get-tuple-element.123) | copy-start | bytes 100
  184.9 14.7 %copy-start.37 = (f32[8]{0:T(128)S(1)}, f32[8]{0:T(128)}, u32[]{:S(2)}) copy-start(f32[8]{0:T(128)} %get-tuple-element.124) | copy-start | bytes 100
  184.9 14.8 %copy-start.36 = (f32[8]{0:T(128)S(1)}, f32[8]{0:T(128)}, u32[]{:S(2)}) copy-start(f32[8]{0:T(128)} %get-tuple-element.125) | copy-start | bytes 100
  184.9 14.9 %copy-start.35 = (f32[8]{0:T(128)S(1)}, f32[8]{0:T(128)}, u32[]{:S(2)}) copy-start(f32[8]{0:T(128)} %get-tuple-element.126) | copy-start | bytes 100
  190.3 19.5 %copy-start.24 = (f32[8,128]{1,0:T(8,128)S(1)}, f32[8,128]{1,0:T(8,128)}, u32[]{:S(2)}) copy-start(f32[8,128]{1,0:T(8,128)} %get-tuple-element.119) | copy-start | bytes 12292
  191.5 2.5 copy-start.6
Sparse Core Ops, SparseCore 0:
  49.5 77.1 all-gather.4
  196.1 91.1 all-reduce.5
where the time goes:
time: 299 us; the launch traced here: 298 us
  blocking collectives  154 us (52%)
  matrix products  60 us (20%)
  waiting for transfers between devices  47 us (16%)
  between operations  15.3 us (5%)
  local copies, waits for them, and re-layouts  12.9 us (4%)
  other arithmetic  8.97 us (3%)
    unnamed x2, blocking collectives  65.4 us
    psum x1, waiting for transfers between devices, on_device(): return lax.psum((grad_query, grad_key, grad_levels, grad_gain), 'seq')  47 us
    psum x1, blocking collectives, on_device(): return lax.psum((grad_query, grad_key, grad_levels, grad_gain), 'seq')  30.6 us
    all_gather x1, blocking collectives, teacher_target(): value_piece = lax.all_gather(value_rows, 'seq', axis=0, tiled=True)  23.8 us
    all_gather x1, blocking collectives, teacher_target(): key_piece = lax.all_gather(key_rows, 'seq', axis=0, tiled=True)  22.4 us
    dot_general x1, matrix products, fenwick_gathered(): jnp.einsum('njg,ngab->jgab', coupling, piece_states, precision=HIGHEST)  12.5 us
    dot_general x1, matrix products, on_device(): jnp.einsum('jgab,gab->gj', level_states, d_combined, precision=HIGHEST)  9.65 us
    unnamed x89, local copies, waits for them, and re-layouts  7.34 us
  transfers between devices with their start and end apart: 2, of which 1 were waited for; matrix products, arithmetic and copies ran while one was open for 9% of the time, Pallas kernels for 0%

commit v1 on v0

--- a/solution.py
+++ b/solution.py
@@ -32,8 +32,11 @@
     score_scale = head_dim ** (-0.5)
     positions = first_row + lax.iota(jnp.int32, span_rows)
     row_peak = jnp.full((head_count, span_rows), NEGATIVE, jnp.float32)
-    key_piece = lax.all_gather(key_rows, "seq", axis=0, tiled=True)
-    value_piece = lax.all_gather(value_rows, "seq", axis=0, tiled=True)
+    key_piece, value_piece = jnp.split(
+        lax.all_gather(jnp.concatenate([key_rows, value_rows], axis=1), "seq", axis=0, tiled=True),
+        [key_rows.shape[1]],
+        axis=1,
+    )
     scores = (
         jnp.einsum("rgd,kd->grk", query_rows, key_piece, preferred_element_type=jnp.float32)
         * score_scale

time: 299 us -> 286 us (0.957)
  blocking collectives: 154 us -> 107 us
  waiting for transfers between devices: 47 us -> 73.6 us
  local copies, waits for them, and re-layouts: 12.9 us -> 17.3 us
    all_gather x2 -> x0, blocking collectives: 46.2 us -> none  [the longest x1 23.8 us: teacher_target(): value_piece = lax.all_gather(value_rows, 'seq', axis=0, tiled=True)]
    all_gather x1, waiting for transfers between devices: 0.01 us -> 25.1 us  [fenwick_gathered(): piece_states = lax.all_gather(raw_state[None], 'seq', axis=0, tiled=True)]
    unnamed x89 -> x87, local copies, waits for them, and re-layouts: 7.34 us -> 11.7 us
  transfers between devices with their start and end apart: 2 -> 3, of which waited for: 1 -> 2; matrix products, arithmetic and copies ran while one was open for 9% -> 12% of each run, Pallas kernels for 0% -> 0%
where the time goes in v1:
time: 286 us; the launch traced here: 285 us
  blocking collectives  107 us (37%)
  waiting for transfers between devices  73.6 us (26%)
  matrix products  62.5 us (22%)
  local copies, waits for them, and re-layouts  17.3 us (6%)
  between operations  15 us (5%)
  other arithmetic  9.22 us (3%)
    unnamed x2, blocking collectives  65.8 us
    psum x1, waiting for transfers between devices, on_device(): return lax.psum((grad_query, grad_key, grad_levels, grad_gain), 'seq')  48.4 us
    psum x1, blocking collectives, on_device(): return lax.psum((grad_query, grad_key, grad_levels, grad_gain), 'seq')  30.8 us
    all_gather x1, waiting for transfers between devices, fenwick_gathered(): piece_states = lax.all_gather(raw_state[None], 'seq', axis=0, tiled=True)  25.1 us
    dot_general x1, matrix products, fenwick_gathered(): jnp.einsum('njg,ngab->jgab', coupling, piece_states, precision=HIGHEST)  12.4 us
    unnamed x87, local copies, waits for them, and re-layouts  11.7 us
    dot_general x1, matrix products, on_device(): jnp.einsum('jgab,gab->gj', level_states, d_combined, precision=HIGHEST)  9.66 us
    dot_general x1, matrix products, teacher_target(): jnp.einsum('grk,kd->grd', weights.astype(jnp.bfloat16), value_piece, pref...  7.11 us
  transfers between devices with their start and end apart: 3, of which 2 were waited for; matrix products, arithmetic and copies ran while one was open for 12% of the time, Pallas kernels for 0%

profile of v1, /device:TPU:0, one launch (start us, length us, event | category | flops | bytes accessed | tf_op | source)
XLA Modules:
  0.0 285.3 jit_solution(17341588087106676626)
XLA Ops:
  7.2 1.5 pad_maximum_fusion
  8.8 1.0 reduce_window_sum.11
  9.8 0.2 slice_reduce_fusion.9
  10.0 1.2 dynamic-slice
  11.9 0.2 dynamic-update-slice
  12.1 35.1 %all-reduce = f32[128]{0:T(128)S(1)} all-reduce(f32[128]{0:T(128)S(1)} %dynamic-update-slice), channel_id=2, replica_groups=mesh['seq'=16,'head'=2] {'seq'}, use_global_device_ids=true, to_apply=%add | all-reduce | flops 128 | bytes 1024
  47.2 0.1 reshape.329
  47.3 0.6 while.14
  47.9 0.8 copy.116
  48.8 0.2 slice_reduce_fusion
  49.1 2.0 fusion.23
  51.1 0.8 slice.46
  51.9 0.2 dynamic-update-slice.1
  52.1 30.7 %all-reduce.1 = f32[128]{0:T(128)S(1)} all-reduce(f32[128]{0:T(128)S(1)} %dynamic-update-slice.1), channel_id=4, replica_groups=mesh['seq'=16,'head'=2] {'seq'}, use_global_device_ids=true, to_apply=%add.1 | all-reduce | flops 128 | bytes 1024
  82.7 0.1 reshape.331
  82.9 1.3 slice_reduce_fusion.8
  84.7 0.6 compare_convert_fusion.8
  85.4 0.7 broadcast_multiply_fusion
  86.1 0.7 select_exponential_fusion.1
  86.7 1.3 fusion.53
  88.1 1.7 fusion.29
  89.8 0.7 fusion.66
  90.6 0.7 copy-done.10
  91.3 2.4 fusion.25
  93.7 0.2 iota_compare_fusion
  94.0 2.5 fusion.4
  96.5 3.2 %copy-done.1 = f32[2048,128,8]{1,0,2:T(8,128)} copy-done((f32[2048,128,8]{1,0,2:T(8,128)}, f32[2048,128,8]{1,0,2:T(8,128)S(1)}, u32[]{:S(2)}) %copy-start.1) | copy-done | bytes 8388632
  99.7 1.7 fusion.2
  101.4 25.1 %all-gather.8.cloned.1.call-done = f32[128,128,128]{2,1,0:T(8,128)} async-done(((f32[8,128,128]{2,1,0:T(8,128)}), f32[128,128,128]{2,1,0:T(8,128)}) %all-gather.8.cloned.1.call-update) | async-done | bytes 8388624 | tf_op jit(solution)/shard_map/all_gather | solution.py:57
  126.5 12.4 %fusion = f32[8,128,128,4]{2,3,1,0:T(4,128)S(1)} fusion(f32[16,8,128,128]{3,2,1,0:T(8,128)} %bitcast.126, f32[16,8]{0,1:T(8,128)} %select_exponential_fusion.1, f32[16,4]{0,1:T(4,128)} %compare_convert_fusion.8), kind=kOutput, calls=%fused_computation.3 | convolution fusion | flops 100663808 | bytes 10486528 | tf_op jit(solution)/shard_map/njg,ngab->jgab/dot_general | solution.py:69
  138.9 4.0 %fusion.10 = f32[8,1,128,128]{3,1,2,0:T(1,128)S(1)} fusion(f32[8,4,1,1]{1,2,3,0:T(1,128)S(1)} %bitcast.129, f32[8,128,128,4]{2,3,1,0:T(4,128)S(1)} %fusion), kind=kOutput, calls=%fused_computation.13 | convolution fusion | flops 6291456 | bytes 2621568 | tf_op jit(solution)/shard_map/gj,jgab->gab/dot_general | solution.py:123
  142.9 0.8 copy-done.2
  143.7 1.0 fusion.67
  144.8 0.8 copy-done.4
  145.6 2.0 multiply_reduce_fusion.10
  147.6 4.9 %psum.42 = f32[128]{0:T(128)S(1)} all-reduce(f32[128]{0:T(128)S(1)} %get-tuple-element.153), channel_id=1, replica_groups=mesh['seq'=16,'head'=2] {'head'}, use_global_device_ids=true, to_apply=%region_4.5 | all-reduce | flops 128 | bytes 1024 | tf_op jit(solution)/shard_map/psum | solution.py:130
  152.5 0.5 copy-done.39
  153.1 7.1 %multiply_reduce_fusion = (f32[8,128]{1,0:T(8,128)S(1)}, f32[128]{0:T(128)}, f32[8,128,128]{2,1,0:T(8,128)}) fusion(f32[8,128,128]{2,1,0:T(8,128)} %get-tuple-element.154, f32[128]{0:T(128)S(1)} %add_rsqrt_fusion, f32[8,128]{1,0:T(8,128)S(1)} %broadcast_multiply_fusion, f32[8,128]{1,0:T(8,128)S(1)} %fusion.2, ...), kind=kOutput, calls=%fused_computation.29 | convolution fusion | flops 546569088 | bytes 10245120 | tf_op jit(solution)/shard_map/grk,kd->grd/dot_general | solution.py:48
  160.2 5.8 %psum.43 = f32[128]{0:T(128)} all-reduce(f32[128]{0:T(128)} %get-tuple-element.120), channel_id=1, replica_groups=mesh['seq'=16,'head'=2] {'head'}, use_global_device_ids=true, to_apply=%region_8.9 | all-reduce | flops 128 | bytes 1024 | tf_op jit(solution)/shard_map/psum | solution.py:137
  165.9 0.8 fusion.63
  166.7 1.3 multiply_subtract_fusion
  168.1 2.7 multiply_reduce_fusion.1
  170.8 2.9 %fusion.36 = f32[8,128,128]{2,1,0:T(8,128)S(1)} fusion(f32[8,128,128]{2,1,0:T(8,128)} %copy-done.7, f32[8,128,128]{2,1,0:T(8,128)S(1)} %get-tuple-element.158, f32[128,128]{1,0:T(8,128)S(1)} %get-tuple-element.160, f32[8]{0:T(128)} %copy-done.30, f32[128,128]{1,0:T(8,128)} %copy-done.19, f32[8]{0:T(128)} %copy-done.24, f32[128,128]{1,0:T(8,128)} %copy-done.20, ...), kind=kOutput, calls=%fused_computation.59 | convolution fusion | flops 203816960 | bytes 2117888 | tf_op jit(solution)/shard_map/grs,gse->gre/dot_general | solution.py:153
  173.7 2.4 fusion.34
  176.2 1.2 fusion.21
  177.3 0.7 fusion.12
  178.0 0.4 convolution_bitcast_fusion
  178.5 1.4 convolution_bitcast_fusion.1
  179.8 2.0 convolution_add_fusion
  181.9 2.1 convolution_bitcast_fusion.2
  183.9 1.3 copy.155
  185.2 0.1 copy.137
  185.3 0.1 copy.138
  185.4 0.1 copy.136
  185.5 0.1 copy.135
  185.6 0.1 copy.134
  185.7 0.1 copy.133
  185.7 0.1 copy.132
  185.9 9.7 %fusion.8 = f32[8,1,4,1]{2,1,3,0:T(1,128)S(1)} fusion(f32[8,128,128,1]{2,3,1,0:T(1,128)} %copy.155, f32[8,128,128,4]{2,3,1,0:T(4,128)S(1)} %fusion), kind=kOutput, calls=%fused_computation.11 | convolution fusion | flops 6291456 | bytes 2621568 | tf_op jit(solution)/shard_map/jgab,gab->gj/dot_general | solution.py:161
  195.6 0.1 concatenate.7
  195.7 30.8 %all-reduce.2 = (f32[8,12]{1,0:T(8,128)}, f32[1024]{0:T(1024)}) all-reduce(f32[8,12]{1,0:T(8,128)S(1)} %concatenate.7, f32[1024]{0:T(1024)S(1)} %bitcast.132), channel_id=1, replica_groups=mesh['seq'=16,'head'=2] {'seq'}, use_global_device_ids=true, to_apply=%region_19.20 | all-reduce | flops 1120 | bytes 8960 | tf_op jit(solution)/shard_map/psum | solution.py:163
  226.4 48.4 %all-reduce.6.cloned.1.call-done = (f32[8,128,128]{1,2,0:T(8,128)}, f32[8,128,128]{2,1,0:T(8,128)}) async-done(((f32[8,128,128]{1,2,0:T(8,128)}, f32[8,128,128]{2,1,0:T(8,128)}), (f32[8,128,128]{1,2,0:T(8,128)}, f32[8,128,128]{2,1,0:T(8,128)})) %all-reduce.6.cloned.1.call-update) | async-done | bytes 1048592 | tf_op jit(solution)/shard_map/psum | solution.py:163
  274.8 2.0 copy.139
  276.9 1.9 copy.186
  (115 shorter events, 1.3 us)
Async XLA Ops:
  7.2 79.6 %copy-start = (f32[8,128,128]{2,1,0:T(8,128)S(1)}, f32[8,128,128]{2,1,0:T(8,128)}, u32[]{:S(2)}) copy-start(f32[8,128,128]{2,1,0:T(8,128)} %param.15) | copy-start | bytes 1572868
  7.2 86.8 %copy-start.8 = (bf16[128,1024]{1,0:T(8,128)(2,1)S(1)}, bf16[128,1024]{1,0:T(8,128)(2,1)}, u32[]{:S(2)}) copy-start(bf16[128,1024]{1,0:T(8,128)(2,1)} %param.10) | copy-start | bytes 786436
  7.2 86.8 %all-gather.6.cloned.1.call-start = ((), (), s32[]{:S(2)}) async-start(), calls=%async_computation | async-start | bytes 1114112 | tf_op jit(solution)/shard_map/all_gather | solution.py:36
  8.7 117.8 %all-gather.8.cloned.1.call-start = ((), (), s32[]{:S(2)}) async-start(), calls=%async_computation.1 | async-start | bytes 8912896 | tf_op jit(solution)/shard_map/all_gather | solution.py:57
  51.1 223.8 %all-reduce.6.cloned.1.call-start = ((), (), s32[]{:S(2)}) async-start(), calls=%async_computation.2 | async-start | bytes 2097152 | tf_op jit(solution)/shard_map/psum | solution.py:163
  84.2 6.3 %copy-start.23 = (f32[8]{0:T(128)}, f32[8]{0:T(128)S(1)}, u32[]{:S(2)}) copy-start(f32[8]{0:T(128)S(1)} %get-tuple-element.129) | copy-start | bytes 100
  84.2 6.3 %copy-start.24 = (f32[8]{0:T(128)}, f32[8]{0:T(128)S(1)}, u32[]{:S(2)}) copy-start(f32[8]{0:T(128)S(1)} %get-tuple-element.130) | copy-start | bytes 100
  84.2 6.3 %copy-start.25 = (f32[8]{0:T(128)}, f32[8]{0:T(128)S(1)}, u32[]{:S(2)}) copy-start(f32[8]{0:T(128)S(1)} %get-tuple-element.131) | copy-start | bytes 100
  84.2 6.3 %copy-start.26 = (f32[8]{0:T(128)}, f32[8]{0:T(128)S(1)}, u32[]{:S(2)}) copy-start(f32[8]{0:T(128)S(1)} %get-tuple-element.132) | copy-start | bytes 100
  84.2 6.3 %copy-start.27 = (f32[8]{0:T(128)}, f32[8]{0:T(128)S(1)}, u32[]{:S(2)}) copy-start(f32[8]{0:T(128)S(1)} %get-tuple-element.133) | copy-start | bytes 100
  84.3 6.3 %copy-start.28 = (f32[8]{0:T(128)}, f32[8]{0:T(128)S(1)}, u32[]{:S(2)}) copy-start(f32[8]{0:T(128)S(1)} %get-tuple-element.134) | copy-start | bytes 100
  84.3 6.3 %copy-start.29 = (f32[8]{0:T(128)}, f32[8]{0:T(128)S(1)}, u32[]{:S(2)}) copy-start(f32[8]{0:T(128)S(1)} %get-tuple-element.135) | copy-start | bytes 100
  84.3 6.3 %copy-start.30 = (f32[8]{0:T(128)}, f32[8]{0:T(128)S(1)}, u32[]{:S(2)}) copy-start(f32[8]{0:T(128)S(1)} %get-tuple-element.136) | copy-start | bytes 100
  84.4 12.1 %copy-start.14 = (f32[128,128]{1,0:T(8,128)}, f32[128,128]{1,0:T(8,128)S(1)}, u32[]{:S(2)}) copy-start(f32[128,128]{1,0:T(8,128)S(1)} %compare_convert_fusion.7) | copy-start | bytes 196612
  84.4 6.2 %copy-start.21 = (pred[128,128]{1,0:T(8,128)(4,1)}, pred[128,128]{1,0:T(8,128)(4,1)S(1)}, u32[]{:S(2)}) copy-start(pred[128,128]{1,0:T(8,128)(4,1)S(1)} %get-tuple-element.159) | copy-start | bytes 49156
  84.5 9.2 %copy-start.15 = (f32[128,128]{1,0:T(8,128)}, f32[128,128]{1,0:T(8,128)S(1)}, u32[]{:S(2)}) copy-start(f32[128,128]{1,0:T(8,128)S(1)} %get-tuple-element.165) | copy-start | bytes 196612
  84.5 9.2 %copy-start.16 = (f32[128,128]{1,0:T(8,128)}, f32[128,128]{1,0:T(8,128)S(1)}, u32[]{:S(2)}) copy-start(f32[128,128]{1,0:T(8,128)S(1)} %get-tuple-element.166) | copy-start | bytes 196612
  84.6 9.1 %copy-start.17 = (f32[128,128]{1,0:T(8,128)}, f32[128,128]{1,0:T(8,128)S(1)}, u32[]{:S(2)}) copy-start(f32[128,128]{1,0:T(8,128)S(1)} %get-tuple-element.163) | copy-start | bytes 196612
  84.6 9.1 %copy-start.18 = (f32[128,128]{1,0:T(8,128)}, f32[128,128]{1,0:T(8,128)S(1)}, u32[]{:S(2)}) copy-start(f32[128,128]{1,0:T(8,128)S(1)} %get-tuple-element.164) | copy-start | bytes 196612
  84.7 9.0 %copy-start.19 = (f32[128,128]{1,0:T(8,128)}, f32[128,128]{1,0:T(8,128)S(1)}, u32[]{:S(2)}) copy-start(f32[128,128]{1,0:T(8,128)S(1)} %get-tuple-element.161) | copy-start | bytes 196612
  84.7 9.0 %copy-start.20 = (f32[128,128]{1,0:T(8,128)}, f32[128,128]{1,0:T(8,128)S(1)}, u32[]{:S(2)}) copy-start(f32[128,128]{1,0:T(8,128)S(1)} %get-tuple-element.162) | copy-start | bytes 196612
  88.1 1.7 copy-start.7
  90.5 0.8 copy-start.10
  93.9 7.5 %copy-start.9 = (pred[128,2048]{0,1:T(8,128)(4,1)}, pred[128,2048]{0,1:T(8,128)(4,1)S(1)}, u32[]{:S(2)}) copy-start(pred[128,2048]{0,1:T(8,128)(4,1)S(1)} %iota_compare_fusion) | copy-start | bytes 786436
  96.5 3.2 %copy-start.1 = (f32[2048,128,8]{1,0,2:T(8,128)}, f32[2048,128,8]{1,0,2:T(8,128)S(1)}, u32[]{:S(2)}) copy-start(f32[2048,128,8]{1,0,2:T(8,128)S(1)} %get-tuple-element.152) | copy-start | bytes 25165828
  126.5 19.1 %copy-start.11 = (f32[8,128,128]{2,1,0:T(8,128)S(1)}, f32[8,128,128]{2,1,0:T(8,128)}, u32[]{:S(2)}) copy-start(f32[8,128,128]{2,1,0:T(8,128)} %fusion.25) | copy-start | bytes 1572868
  126.5 26.5 %copy-start.22 = (f32[1024]{0:T(1024)S(1)}, f32[1024]{0:T(1024)}, u32[]{:S(2)}) copy-start(f32[1024]{0:T(1024)} %param.17) | copy-start | bytes 12292
  142.9 0.8 copy-start.2
  144.8 0.8 copy-start.4
  152.5 0.5 copy-start.39
  152.5 0.5 copy-start.31
  153.1 15.0 %copy-start.13 = (bf16[128,128]{1,0:T(8,128)(2,1)S(1)}, bf16[128,128]{1,0:T(8,128)(2,1)}, u32[]{:S(2)}) copy-start(bf16[128,128]{1,0:T(8,128)(2,1)} %param.12) | copy-start | bytes 98308
  160.2 17.9 %copy-start.12 = (bf16[128,128]{1,0:T(8,128)(2,1)S(1)}, bf16[128,128]{1,0:T(8,128)(2,1)}, u32[]{:S(2)}) copy-start(bf16[128,128]{1,0:T(8,128)(2,1)} %param.11) | copy-start | bytes 98308
  165.9 11.4 %copy-start.5 = (f32[8,128,128]{2,1,0:T(8,128)S(1)}, f32[8,128,128]{2,1,0:T(8,128)}, u32[]{:S(2)}) copy-start(f32[8,128,128]{2,1,0:T(8,128)} %copy-done.4) | copy-start | bytes 1572868
  165.9 13.9 %copy-start.3 = (f32[8,1,128,128]{3,1,2,0:T(1,128)S(1)}, f32[8,1,128,128]{3,1,2,0:T(1,128)}, u32[]{:S(2)}) copy-start(f32[8,1,128,128]{3,1,2,0:T(1,128)} %copy-done.2) | copy-start | bytes 1572868
  170.8 14.5 %copy-start.38 = (f32[8]{0:T(128)S(1)}, f32[8]{0:T(128)}, u32[]{:S(2)}) copy-start(f32[8]{0:T(128)} %get-tuple-element.122) | copy-start | bytes 100
  170.8 14.5 %copy-start.37 = (f32[8]{0:T(128)S(1)}, f32[8]{0:T(128)}, u32[]{:S(2)}) copy-start(f32[8]{0:T(128)} %get-tuple-element.121) | copy-start | bytes 100
  170.8 14.6 %copy-start.36 = (f32[8]{0:T(128)S(1)}, f32[8]{0:T(128)}, u32[]{:S(2)}) copy-start(f32[8]{0:T(128)} %get-tuple-element.123) | copy-start | bytes 100
  170.8 14.7 %copy-start.35 = (f32[8]{0:T(128)S(1)}, f32[8]{0:T(128)}, u32[]{:S(2)}) copy-start(f32[8]{0:T(128)} %get-tuple-element.124) | copy-start | bytes 100
  170.8 14.8 %copy-start.34 = (f32[8]{0:T(128)S(1)}, f32[8]{0:T(128)}, u32[]{:S(2)}) copy-start(f32[8]{0:T(128)} %get-tuple-element.125) | copy-start | bytes 100
  170.8 14.9 %copy-start.33 = (f32[8]{0:T(128)S(1)}, f32[8]{0:T(128)}, u32[]{:S(2)}) copy-start(f32[8]{0:T(128)} %get-tuple-element.126) | copy-start | bytes 100
  170.8 14.9 %copy-start.32 = (f32[8]{0:T(128)S(1)}, f32[8]{0:T(128)}, u32[]{:S(2)}) copy-start(f32[8]{0:T(128)} %get-tuple-element.127) | copy-start | bytes 100
  177.3 2.5 copy-start.6
Sparse Core Ops, SparseCore 0:
  10.2 40.6 all-gather.5
  53.0 73.4 all-gather.7
  182.0 92.7 all-reduce.5
